TPU v7x, 256 devices: a 4x2x16 block of a 4x16x16 slice. The times are simulated.
256 devices in a mesh: pb: 2 (over y), col: 32 (over z, core), row: 4 (over x).
Axes of the slice: x: 4, y: 2, z: 16, core: 2. Of those that a mesh axis runs over, the one named last changes fastest.
The devices are a block of a 4x16x16 slice.
Arguments:
- pair_density: bfloat16 [6144, 6144], P(('pb', 'col'), 'row'), parts along dimension 0, may hold values from -0.19921875 to 0.19921875
- band_pairs: int32 [2, 3072], replicated, may hold values from 0 to 255, as said below
- valence: float32 [256], replicated, may hold values from -12 to -2
- conduction: float32 [12], replicated, may hold values from 1 to 8
- wave_vectors: int32 [3, 12288], P(None, 'pb'), parts along dimension 1, may hold values from -6 to 6
- momentum: float32 [6], P('pb'), parts along dimension 0, may hold values from 0.3 to 0.7
- guess_scale: float32 [12288], P('pb'), parts along dimension 0, may hold values from 0.4 to 0.75
Outputs:
- epsilon: float32 [12288, 6144], P(('pb', 'row'), 'col'), parts along dimension 0
- inverse: float32 [12288, 6144], P(('pb', 'row'), 'col'), parts along dimension 0
There are 2 independent parts, one for each index of `pb`. A program takes and returns all parts, laid end to end along the dimension named above; an argument that names none is the same for every part. Nothing has to cross between parts.
Inputs may be any that keep to these rules, and one draw needn't show every extreme that they name: `band_pairs`: column p names a valence band below 256 in row 0 and a conduction band below 12 in row 1; every such pair of bands appears in exactly one column.
All inputs are finite; a program needn't handle non-finite values.
Results may differ from a plain program's by a relative error of at most 0.0036.
The roundings to bfloat16 on the way count: a program that leaves them out, or rounds other values in their place, can miss the bound.
Values may be sent and summed in bfloat16 or wider, within the bound.
A program may use at most 64 MiB of HBM per device.

v0:
```python
import math
import jax
import jax.numpy as jnp
from jax import lax
from jax.sharding import PartitionSpec as P


def lookup(indices, table):
    levels = jnp.arange(table.shape[0], dtype=jnp.int32)
    picked = indices[:, None] == levels[None, :]
    return jnp.sum(jnp.where(picked, table[None, :], 0.0), axis=1)


def on_device(pair_density, band_pairs, valence, conduction, wave_vectors, momentum, guess_scale):
    column_index = lax.axis_index("col")
    row_index = lax.axis_index("row")
    row_height = pair_density.shape[1]
    whole_width = row_height * lax.axis_size("row")
    strip_width = whole_width // lax.axis_size("col")
    valence_of = lookup(band_pairs[0], valence)
    conduction_of = lookup(band_pairs[1], conduction)
    weight = 4.0 / (valence_of - conduction_of)
    shifted = wave_vectors.astype(jnp.float32) + momentum[:, None]
    sqrt_all = jnp.sqrt(4.0 * math.pi / jnp.sum(shifted * shifted, axis=0))
    row_first = row_index * row_height
    column_first = column_index * strip_width
    sqrt_rows = lax.dynamic_slice_in_dim(sqrt_all, row_first, row_height, 0)
    sqrt_cols = lax.dynamic_slice_in_dim(sqrt_all, column_first, strip_width, 0)
    scale_rows = lax.dynamic_slice_in_dim(guess_scale, row_first, row_height, 0)
    scale_cols = lax.dynamic_slice_in_dim(guess_scale, column_first, strip_width, 0)
    panel_pairs = lax.all_gather(pair_density, "col", axis=0, tiled=True)
    owner = column_first // row_height
    offset = column_first % row_height
    own_slice = lax.dynamic_slice_in_dim(panel_pairs, offset, strip_width, 1)
    candidates = lax.all_gather(own_slice, "row", axis=1, tiled=True)
    strip_pairs = lax.dynamic_slice_in_dim(candidates, owner * strip_width, strip_width, 1)
    weighted = (weight[:, None] * panel_pairs.astype(jnp.float32)).astype(jnp.bfloat16)
    weighted_strip = (weight[:, None] * strip_pairs.astype(jnp.float32)).astype(jnp.bfloat16)
    chi_block = lax.dot_general(
        weighted, strip_pairs, (((0,), (0,)), ((), ())), preferred_element_type=jnp.float32
    )
    chi_rows = jnp.sum(weighted.astype(jnp.float32) * panel_pairs.astype(jnp.float32), axis=0)
    chi_cols = jnp.sum(weighted_strip.astype(jnp.float32) * strip_pairs.astype(jnp.float32), axis=0)
    global_rows = row_first + jnp.arange(row_height, dtype=jnp.int32)
    global_cols = column_first + jnp.arange(strip_width, dtype=jnp.int32)
    identity = (global_rows[:, None] == global_cols[None, :]).astype(jnp.float32)
    epsilon = identity - sqrt_rows[:, None] * chi_block * sqrt_cols[None, :]
    diagonal_rows = 1.0 - sqrt_rows * chi_rows * sqrt_rows
    guess_rows = scale_rows / diagonal_rows
    guess_cols = scale_cols / (1.0 - sqrt_cols * chi_cols * sqrt_cols)
    mixed = epsilon * guess_cols[None, :]
    mixed_b = mixed.astype(jnp.bfloat16)
    mixed_diagonal = diagonal_rows * guess_rows
    rounded_diagonal = mixed_diagonal.astype(jnp.bfloat16).astype(jnp.float32)
    delta = guess_rows + (rounded_diagonal - mixed_diagonal)
    inner = sqrt_rows * guess_rows

    def times_mixed(block):
        wide = block.astype(jnp.float32)
        scaled = (inner[:, None] * wide).astype(jnp.bfloat16)
        partial = jnp.dot(panel_pairs, scaled, preferred_element_type=jnp.float32)
        total = lax.psum(partial.astype(jnp.bfloat16), "row")
        spread = lax.dot_general(
            weighted, total, (((0,), (0,)), ((), ())), preferred_element_type=jnp.float32
        )
        return delta[:, None] * wide - sqrt_rows[:, None] * spread

    square = times_mixed(mixed_b)
    cube = times_mixed(square.astype(jnp.bfloat16))
    inverse = guess_rows[:, None] * (4.0 * identity - 6.0 * mixed + 4.0 * square - cube)
    return (epsilon, inverse)


def solution(mesh):
    placed = (P(("pb", "col"), "row"), P(), P(), P(), P(None, "pb"), P("pb"), P("pb"))
    return jax.shard_map(
        on_device,
        mesh=mesh,
        in_specs=placed,
        out_specs=(P(("pb", "row"), "col"), P(("pb", "row"), "col")),
        check_vma=False,
    )
```

profile of v0, /device:TPU:33, one launch (start us, length us, event | category | flops | bytes accessed | tf_op | source)
XLA Modules:
  0.0 317.8 jit_solution(16853335193049921923)
XLA Ops:
  7.2 0.1 all-gather.3.cloned.1.call-start
  7.2 0.7 all-gather.3.cloned.1.call-update
  8.0 0.1 all-gather.5.cloned.1.call-start
  8.1 94.8 %all-gather.3.cloned.1.call-done = bf16[3072,1536]{1,0:T(8,128)(2,1)} async-done(((bf16[96,1536]{1,0:T(8,128)(2,1)}), bf16[3072,1536]{1,0:T(8,128)(2,1)}) %all-gather.3.cloned.1.call-update) | async-done | bytes 9437200 | tf_op jit(solution)/shard_map/all_gather | solution.py:31
  102.8 2.4 constant_dynamic-slice_fusion
  105.3 1.5 copy.11
  106.8 0.1 all-reduce.3.cloned.1.call-start
  106.9 0.5 copy-done.1
  107.5 0.1 select_reduce_fusion.1
  107.7 0.1 multiply_reduce_fusion
  107.8 1.9 select_reduce_fusion
  109.7 6.2 %fusion.1 = f32[1536]{0:T(1024)S(1)} fusion(bf16[3072,1536]{1,0:T(8,128)(2,1)} %all-gather.3.cloned.1.call-done, f32[3072]{0:T(1024)S(1)} %subtract_divide_fusion), kind=kLoop, calls=%fused_computation.3 | loop fusion | flops 28310016 | bytes 9455616 | tf_op jit(solution)/shard_map/reduce_sum | solution.py:42
  116.0 0.8 subtract_add_fusion
  116.8 44.2 %all-gather.5.cloned.1.call-done = bf16[3072,768]{0,1:T(8,128)(2,1)} async-done(((bf16[3072,192]{0,1:T(8,128)(2,1)}), bf16[3072,768]{0,1:T(8,128)(2,1)}) %all-gather.5.cloned.1.call-update) | async-done | bytes 4718608 | tf_op jit(solution)/shard_map/all_gather | solution.py:35
  161.0 1.8 fusion.11
  162.8 0.8 fusion.24
  163.6 6.5 %fusion.5 = f32[1536,192]{0,1:T(8,128)S(1)} fusion(bf16[3072,768]{0,1:T(8,128)(2,1)} %all-gather.5.cloned.1.call-done, s32[]{:T(128)S(6)} %select_n.39, f32[192]{0:T(256)S(1)} %get-tuple-element.6, f32[1536]{0:T(1024)S(1)} %get-tuple-element.4, s32[1536]{0:T(1024)S(1)} %iota_add_fusion, s32[192]{0:T(256)S(1)} %iota_add_fusion.1, ...), kind=kOutput, calls=%fused_computation.16 | convolution fusion | flops 1827569664 | bytes 11822596 | tf_op jit(solution)/shard_map/dot_general | solution.py:39
  170.1 4.3 %fusion.2 = bf16[3072,192]{0,1:T(8,128)(2,1)} fusion(bf16[3072,1536]{1,0:T(8,128)(2,1)S(1)} %bitcast.11, f32[1536]{0:T(1024)S(1)} %mul.163, f32[1536,192]{0,1:T(8,128)S(1)} %fusion.5, f32[192]{0:T(256)S(1)} %get-tuple-element.5), kind=kOutput, calls=%fused_computation.6 | convolution fusion | flops 1814003712 | bytes 11803392 | tf_op jit(solution)/shard_map/dot_general | solution.py:61
  174.4 0.2 all-reduce.5.cloned.1.call-start
  174.7 58.0 %all-reduce.3.cloned.1.call-done = bf16[3072,192]{0,1:T(8,128)(2,1)} async-done(((bf16[3072,192]{0,1:T(8,128)(2,1)}), bf16[3072,192]{0,1:T(8,128)(2,1)}) %all-reduce.3.cloned.1.call-update) | async-done | bytes 1179664 | tf_op jit(solution)/shard_map/psum | solution.py:62
  232.7 6.5 %fusion.6 = f32[1536,192]{0,1:T(8,128)S(1)} fusion(bf16[3072,192]{0,1:T(8,128)(2,1)} %all-reduce.3.cloned.1.call-done, f32[1536]{0:T(1024)S(1)} %get-tuple-element.2, f32[1536]{0:T(1024)S(1)} %get-tuple-element.4, f32[1536,192]{0,1:T(8,128)S(1)} %fusion.5, f32[192]{0:T(256)S(1)} %get-tuple-element.5, bf16[3072,1536]{1,0:T(8,128)(2,1)} %all-gather.3.cloned.1.call-done, ...), kind=kOutput, calls=%fused_computation.17 | convolution fusion | flops 1827864576 | bytes 13001472 | tf_op jit(solution)/shard_map/dot_general | solution.py:63
  239.3 4.2 %fusion.3 = bf16[3072,192]{0,1:T(8,128)(2,1)} fusion(bf16[3072,1536]{1,0:T(8,128)(2,1)S(1)} %bitcast.13, f32[1536]{0:T(1024)S(1)} %mul.163, f32[1536,192]{0,1:T(8,128)S(1)} %fusion.6), kind=kOutput, calls=%fused_computation.7 | convolution fusion | flops 1813708800 | bytes 11802624 | tf_op jit(solution)/shard_map/dot_general | solution.py:61
  243.6 59.8 %all-reduce.5.cloned.1.call-done = bf16[3072,192]{0,1:T(8,128)(2,1)} async-done(((bf16[3072,192]{0,1:T(8,128)(2,1)}), bf16[3072,192]{0,1:T(8,128)(2,1)}) %all-reduce.5.cloned.1.call-update) | async-done | bytes 1179664 | tf_op jit(solution)/shard_map/psum | solution.py:62
  303.4 7.8 %fusion.9 = f32[1536,192]{0,1:T(8,128)} fusion(bf16[3072,192]{0,1:T(8,128)(2,1)} %all-reduce.5.cloned.1.call-done, f32[1536,192]{0,1:T(8,128)S(1)} %fusion.6, f32[1536,192]{0,1:T(8,128)S(1)} %fusion.5, f32[1536]{0:T(1024)S(1)} %get-tuple-element.2, f32[192]{0:T(256)S(1)} %get-tuple-element.5, f32[1536]{0:T(1024)S(1)} %get-tuple-element.3, ...), kind=kOutput, calls=%fused_computation.20 | convolution fusion | flops 1830223872 | bytes 14194176 | tf_op jit(solution)/shard_map/dot_general | solution.py:63
  (34 shorter events, 0.3 us)
Async XLA Ops:
  7.2 95.7 %all-gather.3.cloned.1.call-start = ((), (), s32[]{:S(2)}) async-start(), calls=%async_computation | async-start | bytes 9732096 | tf_op jit(solution)/shard_map/all_gather | solution.py:31
  8.0 153.0 %all-gather.5.cloned.1.call-start = ((), (), s32[]{:S(2)}) async-start(), calls=%async_computation.1 | async-start | bytes 5898240 | tf_op jit(solution)/shard_map/all_gather | solution.py:35
  106.7 0.7 copy-start.1
  106.7 0.8 copy-start.4
  106.7 0.9 copy-start
  106.7 0.9 copy-start.3
  106.8 1.1 copy-start.2
  106.8 125.9 %all-reduce.3.cloned.1.call-start = ((), (), s32[]{:S(2)}) async-start(), calls=%async_computation.2 | async-start | bytes 2359296 | tf_op jit(solution)/shard_map/psum | solution.py:62
  161.0 9.1 %slice-start = ((s8[9437184]{0:T(1024)(128)(4,1)}), s8[4194304]{0:T(1024)(128)(4,1)S(1)}, s32[]{:S(2)}) async-start(s8[9437184]{0:T(1024)(128)(4,1)} %bitcast.10), calls=%async_computation.4 | async-start | bytes 8388608
  163.6 6.5 %slice-start.1 = ((s8[9437184]{0:T(1024)(128)(4,1)}), s8[4194304]{0:T(1024)(128)(4,1)S(1)}, s32[]{:S(2)}) async-start(s8[9437184]{0:T(1024)(128)(4,1)} %bitcast.10), calls=%async_computation.5 | async-start | bytes 8388608
  163.6 6.5 %slice-start.2 = ((s8[9437184]{0:T(1024)(128)(4,1)}), s8[1048576]{0:T(1024)(128)(4,1)S(1)}, s32[]{:S(2)}) async-start(s8[9437184]{0:T(1024)(128)(4,1)} %bitcast.10), calls=%async_computation.6 | async-start | bytes 2097152
  170.1 133.4 %copy-start.5 = (f32[1536,192]{0,1:T(8,128)}, f32[1536,192]{0,1:T(8,128)S(1)}, u32[]{:S(2)}) copy-start(f32[1536,192]{0,1:T(8,128)S(1)} %fusion.5) | copy-start | bytes 3538948
  174.4 64.9 %slice-start.3 = ((s8[9437184]{0:T(1024)(128)(4,1)}), s8[1048576]{0:T(1024)(128)(4,1)S(1)}, s32[]{:S(2)}) async-start(s8[9437184]{0:T(1024)(128)(4,1)} %bitcast.12), calls=%async_computation.7 | async-start | bytes 2097152
  174.4 129.0 %all-reduce.5.cloned.1.call-start = ((), (), s32[]{:S(2)}) async-start(), calls=%async_computation.3 | async-start | bytes 2359296 | tf_op jit(solution)/shard_map/psum | solution.py:62
  232.7 6.5 %slice-start.4 = ((s8[9437184]{0:T(1024)(128)(4,1)}), s8[4194304]{0:T(1024)(128)(4,1)S(1)}, s32[]{:S(2)}) async-start(s8[9437184]{0:T(1024)(128)(4,1)} %bitcast.12), calls=%async_computation.8 | async-start | bytes 8388608
  232.7 6.5 %slice-start.5 = ((s8[9437184]{0:T(1024)(128)(4,1)}), s8[4194304]{0:T(1024)(128)(4,1)S(1)}, s32[]{:S(2)}) async-start(s8[9437184]{0:T(1024)(128)(4,1)} %bitcast.12), calls=%async_computation.9 | async-start | bytes 8388608
Sparse Core Ops, SparseCore 0:
  9.9 92.9 all-gather.2
  106.9 53.9 all-gather.4
  174.6 58.1 all-reduce.2
  243.7 59.6 all-reduce.4
where the time goes:
time: 318 us
  waiting for transfers between devices  258 us (81%)
  matrix products  29.3 us (9%)
  between operations  14 us (4%)
  other arithmetic  11.8 us (4%)
  local copies, waits for them, and re-layouts  4.54 us (1%)
    psum x2, waiting for transfers between devices, times_mixed(): total = lax.psum(partial.astype(jnp.bfloat16), 'row')  118 us
    all_gather x1, waiting for transfers between devices, on_device(): panel_pairs = lax.all_gather(pair_density, 'col', axis=0, tiled=True)  94.8 us
    all_gather x1, waiting for transfers between devices, on_device(): candidates = lax.all_gather(own_slice, 'row', axis=1, tiled=True)  44.2 us
    dot_general x2, matrix products, times_mixed(): lax.dot_general(weighted, total, (((0,), (0,)), ((), ())), preferred_elem...  14.3 us
    dot_general x2, matrix products, times_mixed(): partial = jnp.dot(panel_pairs, scaled, preferred_element_type=jnp.float32)  8.49 us
    dot_general x1, matrix products, on_device(): lax.dot_general(weighted, strip_pairs, (((0,), (0,)), ((), ())), preferre...  6.49 us
  transfers between devices with their start and end apart: 4, of which 4 were waited for; matrix products, arithmetic and copies ran while one was open for 3% of the time, Pallas kernels for 0%

commit v1 on v0

--- a/solution.py
+++ b/solution.py
@@ -59,7 +59,7 @@
         wide = block.astype(jnp.float32)
         scaled = (inner[:, None] * wide).astype(jnp.bfloat16)
         partial = jnp.dot(panel_pairs, scaled, preferred_element_type=jnp.float32)
-        total = lax.psum(partial.astype(jnp.bfloat16), "row")
+        total = jnp.sum(lax.all_gather(partial.astype(jnp.bfloat16), "row"), axis=0)
         spread = lax.dot_general(
             weighted, total, (((0,), (0,)), ((), ())), preferred_element_type=jnp.float32
         )

time: 318 us -> 352 us (1.11)
  local copies, waits for them, and re-layouts: 4.54 us -> 22 us
  other arithmetic: 11.8 us -> 28 us
    all_gather x0 -> x2, waiting for transfers between devices: none -> 118 us  [times_mixed(): total = jnp.sum(lax.all_gather(partial.astype(jnp.bfloat16), 'row'), axis=0)]
    psum x2 -> x0, waiting for transfers between devices: 118 us -> none  [times_mixed(): total = lax.psum(partial.astype(jnp.bfloat16), 'row')]
    all_gather x0 -> x2, local copies, waits for them, and re-layouts: none -> 16.4 us  [times_mixed(): total = jnp.sum(lax.all_gather(partial.astype(jnp.bfloat16), 'row'), axis=0)]
    reduce_sum x0 -> x2, other arithmetic: none -> 16.2 us  [times_mixed(): total = jnp.sum(lax.all_gather(partial.astype(jnp.bfloat16), 'row'), axis=0)]
where the time goes in v1:
time: 352 us
  waiting for transfers between devices  258 us (73%)
  matrix products  29.2 us (8%)
  other arithmetic  28 us (8%)
  local copies, waits for them, and re-layouts  22 us (6%)
  between operations  14 us (4%)
    all_gather x2, waiting for transfers between devices, times_mixed(): total = jnp.sum(lax.all_gather(partial.astype(jnp.bfloat16), 'row'), axis=0)  118 us
    all_gather x1, waiting for transfers between devices, on_device(): panel_pairs = lax.all_gather(pair_density, 'col', axis=0, tiled=True)  94.8 us
    all_gather x1, waiting for transfers between devices, on_device(): candidates = lax.all_gather(own_slice, 'row', axis=1, tiled=True)  44.2 us
    all_gather x2, local copies, waits for them, and re-layouts, times_mixed(): total = jnp.sum(lax.all_gather(partial.astype(jnp.bfloat16), 'row'), axis=0)  16.4 us
    reduce_sum x2, other arithmetic, times_mixed(): total = jnp.sum(lax.all_gather(partial.astype(jnp.bfloat16), 'row'), axis=0)  16.2 us
    dot_general x2, matrix products, times_mixed(): lax.dot_general(weighted, total, (((0,), (0,)), ((), ())), preferred_elem...  14.2 us
    dot_general x2, matrix products, times_mixed(): partial = jnp.dot(panel_pairs, scaled, preferred_element_type=jnp.float32)  8.5 us
  transfers between devices with their start and end apart: 4, of which 4 were waited for; matrix products, arithmetic and copies ran while one was open for 3% of the time, Pallas kernels for 0%

profile of v1, /device:TPU:33, one launch (start us, length us, event | category | flops | bytes accessed | tf_op | source)
XLA Modules:
  0.0 351.7 jit_solution(10672955025727707169)
XLA Ops:
  7.2 0.7 all-gather.7.cloned.1.call-update
  8.1 94.8 %all-gather.7.cloned.1.call-done = bf16[3072,1536]{1,0:T(8,128)(2,1)} async-done(((bf16[96,1536]{1,0:T(8,128)(2,1)}), bf16[3072,1536]{1,0:T(8,128)(2,1)}) %all-gather.7.cloned.1.call-update) | async-done | bytes 9437200 | tf_op jit(solution)/shard_map/all_gather | solution.py:31
  102.8 2.4 constant_dynamic-slice_fusion
  105.3 1.5 copy.11
  106.9 0.5 copy-done.1
  107.8 1.9 select_reduce_fusion
  109.7 6.2 %fusion.1 = f32[1536]{0:T(1024)S(1)} fusion(bf16[3072,1536]{1,0:T(8,128)(2,1)} %all-gather.7.cloned.1.call-done, f32[3072]{0:T(1024)S(1)} %subtract_divide_fusion), kind=kLoop, calls=%fused_computation.3 | loop fusion | flops 28310016 | bytes 9455616 | tf_op jit(solution)/shard_map/reduce_sum | solution.py:42
  116.0 0.8 subtract_add_fusion
  116.8 44.2 %all-gather.9.cloned.1.call-done = bf16[3072,768]{0,1:T(8,128)(2,1)} async-done(((bf16[3072,192]{0,1:T(8,128)(2,1)}), bf16[3072,768]{0,1:T(8,128)(2,1)}) %all-gather.9.cloned.1.call-update) | async-done | bytes 4718608 | tf_op jit(solution)/shard_map/all_gather | solution.py:35
  161.0 1.8 fusion.11
  162.8 0.8 fusion.24
  163.6 6.5 %fusion.5 = f32[1536,192]{0,1:T(8,128)S(1)} fusion(bf16[3072,768]{0,1:T(8,128)(2,1)} %all-gather.9.cloned.1.call-done, s32[]{:T(128)S(6)} %select_n.39, f32[192]{0:T(256)S(1)} %get-tuple-element.6, f32[1536]{0:T(1024)S(1)} %get-tuple-element.4, s32[1536]{0:T(1024)S(1)} %iota_add_fusion, s32[192]{0:T(256)S(1)} %iota_add_fusion.1, ...), kind=kOutput, calls=%fused_computation.16 | convolution fusion | flops 1827569664 | bytes 11822596 | tf_op jit(solution)/shard_map/dot_general | solution.py:39
  170.1 4.3 %fusion.2 = bf16[3072,192]{0,1:T(8,128)(2,1)} fusion(bf16[3072,1536]{1,0:T(8,128)(2,1)S(1)} %bitcast.15, f32[1536]{0:T(1024)S(1)} %mul.163, f32[1536,192]{0,1:T(8,128)S(1)} %fusion.5, f32[192]{0:T(256)S(1)} %get-tuple-element.5), kind=kOutput, calls=%fused_computation.6 | convolution fusion | flops 1814003712 | bytes 11803392 | tf_op jit(solution)/shard_map/dot_general | solution.py:61
  174.4 0.2 all-gather.13.cloned.1.call-start
  174.7 59.0 %all-gather.11.cloned.1.call-done = bf16[12288,192]{0,1:T(8,128)(2,1)} async-done(((bf16[3072,192]{0,1:T(8,128)(2,1)}), bf16[12288,192]{0,1:T(8,128)(2,1)}) %all-gather.11.cloned.1.call-update) | async-done | bytes 4718608 | tf_op jit(solution)/shard_map/all_gather | solution.py:62
  233.7 8.2 %reshape.29 = bf16[4,3072,192]{1,0,2:T(4,128)(2,1)} reshape(bf16[12288,192]{0,1:T(8,128)(2,1)} %all-gather.11.cloned.1.call-done) | data formatting | bytes 9437184 | tf_op jit(solution)/shard_map/all_gather | solution.py:62
  241.9 8.1 %reduce_sum.74 = bf16[3072,192]{0,1:T(8,128)(2,1)S(1)} reduce(bf16[4,3072,192]{1,0,2:T(4,128)(2,1)} %reshape.29, bf16[]{:T(256)} %constant.49.clone.1), dimensions={0}, to_apply=%region_5.6 | reduce | flops 1769472 | bytes 5898242 | tf_op jit(solution)/shard_map/reduce_sum | solution.py:62
  250.1 6.1 %fusion.6 = f32[1536,192]{0,1:T(8,128)S(1)} fusion(bf16[3072,192]{0,1:T(8,128)(2,1)S(1)} %reduce_sum.74, f32[1536]{0:T(1024)S(1)} %get-tuple-element.2, f32[1536]{0:T(1024)S(1)} %get-tuple-element.4, f32[1536,192]{0,1:T(8,128)S(1)} %fusion.5, f32[192]{0:T(256)S(1)} %get-tuple-element.5, bf16[3072,1536]{1,0:T(8,128)(2,1)} %all-gather.7.cloned.1.call-done, ...), kind=kOutput, calls=%fused_computation.17 | convolution fusion | flops 1827864576 | bytes 13001472 | tf_op jit(solution)/shard_map/dot_general | solution.py:63
  256.2 1.0 copy-done.6
  257.2 4.2 %fusion.3 = bf16[3072,192]{0,1:T(8,128)(2,1)} fusion(bf16[3072,1536]{1,0:T(8,128)(2,1)S(1)} %bitcast.17, f32[1536]{0:T(1024)S(1)} %mul.163, f32[1536,192]{0,1:T(8,128)S(1)} %fusion.6), kind=kOutput, calls=%fused_computation.7 | convolution fusion | flops 1813708800 | bytes 11802624 | tf_op jit(solution)/shard_map/dot_general | solution.py:61
  261.5 59.2 %all-gather.13.cloned.1.call-done = bf16[12288,192]{0,1:T(8,128)(2,1)} async-done(((bf16[3072,192]{0,1:T(8,128)(2,1)}), bf16[12288,192]{0,1:T(8,128)(2,1)}) %all-gather.13.cloned.1.call-update) | async-done | bytes 4718608 | tf_op jit(solution)/shard_map/all_gather | solution.py:62
  320.8 8.2 %reshape.30 = bf16[4,3072,192]{1,0,2:T(4,128)(2,1)} reshape(bf16[12288,192]{0,1:T(8,128)(2,1)} %all-gather.13.cloned.1.call-done) | data formatting | bytes 9437184 | tf_op jit(solution)/shard_map/all_gather | solution.py:62
  329.0 8.1 %reduce_sum.75 = bf16[3072,192]{0,1:T(8,128)(2,1)S(1)} reduce(bf16[4,3072,192]{1,0,2:T(4,128)(2,1)} %reshape.30, bf16[]{:T(256)} %constant.49.clone.1), dimensions={0}, to_apply=%region_6.7 | reduce | flops 1769472 | bytes 5898242 | tf_op jit(solution)/shard_map/reduce_sum | solution.py:62
  337.1 8.1 %fusion.9 = f32[1536,192]{0,1:T(8,128)} fusion(bf16[3072,192]{0,1:T(8,128)(2,1)S(1)} %reduce_sum.75, f32[1536,192]{0,1:T(8,128)} %copy-done.6, f32[1536,192]{0,1:T(8,128)S(1)} %fusion.5, f32[1536]{0:T(1024)S(1)} %get-tuple-element.2, f32[192]{0:T(256)S(1)} %get-tuple-element.5, f32[1536]{0:T(1024)S(1)} %get-tuple-element.3, f32[1536]{0:T(1024)S(1)} %get-tuple-element.4, ...), kind=kOutput, calls=%fused_computation.20 | convolution fusion | flops 1830223872 | bytes 14194176 | tf_op jit(solution)/shard_map/dot_general | solution.py:63
  (40 shorter events, 0.7 us)
Async XLA Ops:
  7.2 95.7 %all-gather.7.cloned.1.call-start = ((), (), s32[]{:S(2)}) async-start(), calls=%async_computation | async-start | bytes 9732096 | tf_op jit(solution)/shard_map/all_gather | solution.py:31
  8.0 153.0 %all-gather.9.cloned.1.call-start = ((), (), s32[]{:S(2)}) async-start(), calls=%async_computation.1 | async-start | bytes 5898240 | tf_op jit(solution)/shard_map/all_gather | solution.py:35
  106.7 0.7 copy-start.1
  106.7 0.8 copy-start.4
  106.7 0.9 copy-start
  106.7 0.9 copy-start.3
  106.8 1.1 copy-start.2
  106.8 126.8 %all-gather.11.cloned.1.call-start = ((), (), s32[]{:S(2)}) async-start(), calls=%async_computation.2 | async-start | bytes 5898240 | tf_op jit(solution)/shard_map/all_gather | solution.py:62
  161.0 9.1 %slice-start = ((s8[9437184]{0:T(1024)(128)(4,1)}), s8[4194304]{0:T(1024)(128)(4,1)S(1)}, s32[]{:S(2)}) async-start(s8[9437184]{0:T(1024)(128)(4,1)} %bitcast.14), calls=%async_computation.4 | async-start | bytes 8388608
  163.6 6.5 %slice-start.1 = ((s8[9437184]{0:T(1024)(128)(4,1)}), s8[4194304]{0:T(1024)(128)(4,1)S(1)}, s32[]{:S(2)}) async-start(s8[9437184]{0:T(1024)(128)(4,1)} %bitcast.14), calls=%async_computation.5 | async-start | bytes 8388608
  163.6 6.5 %slice-start.2 = ((s8[9437184]{0:T(1024)(128)(4,1)}), s8[1048576]{0:T(1024)(128)(4,1)S(1)}, s32[]{:S(2)}) async-start(s8[9437184]{0:T(1024)(128)(4,1)} %bitcast.14), calls=%async_computation.6 | async-start | bytes 2097152
  170.1 167.0 %copy-start.5 = (f32[1536,192]{0,1:T(8,128)}, f32[1536,192]{0,1:T(8,128)S(1)}, u32[]{:S(2)}) copy-start(f32[1536,192]{0,1:T(8,128)S(1)} %fusion.5) | copy-start | bytes 3538948
  174.4 146.3 %all-gather.13.cloned.1.call-start = ((), (), s32[]{:S(2)}) async-start(), calls=%async_computation.3 | async-start | bytes 5898240 | tf_op jit(solution)/shard_map/all_gather | solution.py:62
  241.9 15.3 %slice-start.3 = ((s8[9437184]{0:T(1024)(128)(4,1)}), s8[1048576]{0:T(1024)(128)(4,1)S(1)}, s32[]{:S(2)}) async-start(s8[9437184]{0:T(1024)(128)(4,1)} %bitcast.16), calls=%async_computation.7 | async-start | bytes 2097152
  250.0 7.2 %slice-start.4 = ((s8[9437184]{0:T(1024)(128)(4,1)}), s8[4194304]{0:T(1024)(128)(4,1)S(1)}, s32[]{:S(2)}) async-start(s8[9437184]{0:T(1024)(128)(4,1)} %bitcast.16), calls=%async_computation.8 | async-start | bytes 8388608
  250.0 7.2 %slice-start.5 = ((s8[9437184]{0:T(1024)(128)(4,1)}), s8[4194304]{0:T(1024)(128)(4,1)S(1)}, s32[]{:S(2)}) async-start(s8[9437184]{0:T(1024)(128)(4,1)} %bitcast.16), calls=%async_computation.9 | async-start | bytes 8388608
  256.2 1.0 copy-start.6
Sparse Core Ops, SparseCore 0:
  9.9 92.9 all-gather.6
  106.9 53.9 all-gather.8
  174.6 59.0 all-gather.10
  261.7 59.0 all-gather.12
